TPU v7x, 32 devices: a whole 2x2x4 slice. The times are simulated.
32 devices in a mesh: grp: 2 (over x), rep: 8 (over z, y), blk: 2 (over core).
Axes of the slice: x: 2, y: 2, z: 4, core: 2. Of those that a mesh axis runs over, the one named last changes fastest.
Arguments:
- factors: float32 [16, 1280, 1280], P('grp', ('blk', 'rep')), as said below
- damping: float32 [16], P('grp'), may hold values from 0.1 to 1
Outputs:
- root: float32 [16, 1280, 1280], P('grp', ('blk', 'rep'))
- inv_root: float32 [16, 1280, 1280], P('grp', ('blk', 'rep'))
Inputs may be any that keep to these rules, and one draw needn't show every extreme that they name: `factors`: every factor is symmetric positive semidefinite.
All inputs are finite; a program needn't handle non-finite values.
Results may differ from a plain program's by a relative error of at most 0.0035.
The roundings to bfloat16 on the way count: a program that leaves them out, or rounds other values in their place, can miss the bound.
Values may be sent and summed in bfloat16 or wider, within the bound.
A program may use at most 128 MiB of HBM per device.

v0:
```python
import functools

import jax
import jax.numpy as jnp
from jax import lax
from jax.experimental import pallas as pl
from jax.experimental.pallas import tpu as pltpu
from jax.sharding import PartitionSpec as P

ITERS = 4
LANES = 128
CHUNK = 256
MESH = pl.DeviceIdType.MESH


def kernel(
    reps, fac_hbm, damp_ref,
    root_ref, inv_ref, norm_ref,
    fac, part, scale, send_buf, full, step, last_root,
    load_sem, sum_send, sum_recv, in_send, in_recv, fwd_send, fwd_recv,
    ex_send, ex_recv, root_send, root_recv, inv_send, inv_recv,
):
    grp = lax.axis_index("grp")
    rep = lax.axis_index("rep")
    blk = lax.axis_index("blk")
    facs, rows, order = fac.shape
    half = rows * reps
    members = 2 * reps
    rank = blk * reps + rep
    chunks = order // CHUNK
    f32, bf16 = jnp.float32, jnp.bfloat16

    def remote(src, dst, send, recv, r, b):
        return pltpu.make_async_remote_copy(
            src_ref=src, dst_ref=dst, send_sem=send, recv_sem=recv,
            device_id=(grp, r, b), device_id_type=MESH,
        )

    def member(j):
        q = lax.rem(rank + j, members)
        return lax.rem(q, reps), q // reps

    loads = [
        pltpu.make_async_copy(fac_hbm.at[f], fac.at[f], load_sem.at[f]) for f in range(facs)
    ]
    for load in loads:
        load.start()
    barrier = pltpu.get_barrier_semaphore()
    for j in range(1, members):
        r, b = member(j)
        pl.semaphore_signal(barrier, inc=1, device_id=(grp, r, b), device_id_type=MESH)

    row_ids = rank * rows + lax.broadcasted_iota(jnp.int32, (rows, order), 0)
    diag = row_ids == lax.broadcasted_iota(jnp.int32, (rows, order), 1)

    def damped(f):
        return fac[f] + jnp.where(diag, damp_ref[f], 0.0)

    for f in range(facs):
        loads[f].wait()
        x = damped(f)
        col = jnp.sum(x * x, axis=0, keepdims=True)
        acc = col[:, :LANES]
        for c in range(1, order // LANES):
            acc = acc + col[:, c * LANES : (c + 1) * LANES]
        part[pl.ds(rank, 1), f : f + 1, :] = acc[None]
    pl.semaphore_wait(barrier, members - 1)

    sums = []
    for j in range(1, members):
        r, b = member(j)
        copy = remote(part.at[rank], part.at[rank], sum_send.at[j], sum_recv.at[j], r, b)
        copy.start()
        sums.append(copy)
    for copy in sums:
        copy.wait()
    total = part[0]
    for q in range(1, members):
        total = total + part[q]
    norm = jnp.sqrt(jnp.sum(total, axis=1, keepdims=True))
    norm_ref[...] = jnp.broadcast_to(norm, norm_ref.shape)
    scale[...] = jnp.broadcast_to(1.0 / norm, scale.shape)

    y0, z1 = full.at[0], full.at[1]

    def block_rows(b, r):
        return pl.ds(pl.multiple_of((b * reps + r) * rows, rows), rows)

    side_reps = reps // 2
    side = rep // side_reps
    wide = -(-(half // 2) // LANES) * LANES
    narrow = half - wide

    def target(k):
        if k <= side_reps:
            return (1 - side) * side_reps + lax.rem(rep + k, side_reps)
        return side * side_reps + lax.rem(rep + k, side_reps)

    def source(k):
        if k == 0:
            return rep
        back = lax.rem(rep - k + reps, side_reps)
        if k <= side_reps:
            return (1 - side) * side_reps + back
        return side * side_reps + back

    tiles = half // LANES
    widths = sorted({tiles - (r * rows) // LANES for r in range(side_reps, reps)})

    def width_of(r, owner_side):
        mirrored = r + owner_side * (reps - 1 - 2 * r)
        return tiles - (mirrored * rows) // LANES

    def pieces(k, src, owner_side):
        if k == 0 or k > side_reps:
            return [(None, [pl.ds(0, order)])]
        options = []
        for w in widths:
            first = (1 - owner_side) * (half - w * LANES)
            options.append((
                width_of(src, owner_side) == w,
                [pl.ds(pl.multiple_of(h * half + first, LANES), w * LANES) for h in range(2)],
            ))
        return options

    def each(options, act):
        for condition, columns in options:
            if condition is None:
                act(columns)
            else:
                pl.when(condition)(functools.partial(act, columns))

    own_rows = block_rows(blk, rep)

    def in_copy(k, i, c):
        return remote(
            send_buf.at[k, :, c], y0.at[own_rows, c],
            in_send.at[k, i], in_recv.at[k, i], target(k), blk,
        )

    def send_in(k, columns):
        for i, c in enumerate(columns):
            in_copy(k, i, c).start()

    def wait_in(k, columns):
        for i, c in enumerate(columns):
            in_copy(k, i, c).wait_send()

    for k in range(1, reps):
        p = target(k)
        send_buf[k] = (damped(p) * scale[pl.ds(p, 1), 0:1]).astype(bf16)
        each(pieces(k, rep, 1 - side), functools.partial(send_in, k))
    y0[own_rows, :] = (damped(rep) * scale[pl.ds(rep, 1), 0:1]).astype(bf16)

    def forward_copy(k, i, c):
        at = block_rows(blk, source(k))
        return remote(
            y0.at[at, c], y0.at[at, c], fwd_send.at[k, i], fwd_recv.at[k, i], rep, 1 - blk
        )

    def forward(k, columns):
        for i, c in enumerate(columns):
            if k:
                in_copy(k, i, c).wait_recv()
            forward_copy(k, i, c).start()

    def wait_forward(k, columns):
        for i, c in enumerate(columns):
            forward_copy(k, i, c).wait()

    for k in [0] + list(range(side_reps + 1, reps)) + list(range(1, side_reps + 1)):
        each(pieces(k, source(k), side), functools.partial(forward, k))
    for k in range(reps):
        each(pieces(k, source(k), side), functools.partial(wait_forward, k))

    far = half // 2
    miss = half - min(widths) * LANES

    def fill(t, old, row0, col0, mirrored):
        shape = (far, miss)
        r = (row0 + lax.broadcasted_iota(jnp.int32, shape, 0)) // rows
        c = (col0 + lax.broadcasted_iota(jnp.int32, shape, 1)) // LANES
        if mirrored:
            gone = c >= tiles - ((reps - 1 - r) * rows) // LANES
        else:
            gone = c < (r * rows) // LANES
        return jnp.where(gone, t, old.astype(f32)).astype(bf16)

    @pl.when(side == 0)
    def _():
        for hi in range(2):
            for hj in range(2):
                t = y0[hj * half : hj * half + miss, hi * half + narrow : (hi + 1) * half]
                at = (slice(hi * half + far, (hi + 1) * half), slice(hj * half, hj * half + miss))
                t = t.astype(f32).T[far - narrow :, :]
                y0[at] = fill(t, y0[at], far, 0, False)

    @pl.when(side == 1)
    def _():
        for hi in range(2):
            for hj in range(2):
                t = y0[(hj + 1) * half - miss : (hj + 1) * half, hi * half : hi * half + wide]
                at = (slice(hi * half, hi * half + far), slice((hj + 1) * half - miss, (hj + 1) * half))
                t = t.astype(f32).T[:far, :]
                y0[at] = fill(t, y0[at], 0, half - miss, True)

    for q in range(members):
        at = slice(q * rows, (q + 1) * rows)
        ids = q * rows + lax.broadcasted_iota(jnp.int32, (rows, order), 0)
        eye = ids == lax.broadcasted_iota(jnp.int32, (rows, order), 1)
        z1[at, :] = ((jnp.where(eye, 3.0, 0.0) - y0[at, :].astype(f32)) * 0.5).astype(bf16)

    mine = pl.ds(pl.multiple_of(blk * half, half), half)
    pending = []

    def cols(n):
        return slice(n * CHUNK, (n + 1) * CHUNK)

    def share(dst, ex, n):
        view = dst.at[mine, pl.ds(n * CHUNK, CHUNK)]
        copy = remote(view, view, ex_send.at[ex, n], ex_recv.at[ex, n], rep, 1 - blk)
        copy.start()
        pending.append(copy)
        return copy

    def product(lhs, rhs, arrivals, n):
        if arrivals is not None:
            arrivals[n].wait_recv()
        return jnp.dot(lhs, rhs[:, cols(n)], preferred_element_type=f32)

    def advance(lhs, rhs, arrivals, dst, ex):
        shared = []
        for n in range(chunks):
            dst[mine, cols(n)] = product(lhs[...], rhs, arrivals, n).astype(bf16)
            shared.append(share(dst, ex, n))
        return shared

    eye_rows = blk * half + lax.broadcasted_iota(jnp.int32, (half, CHUNK), 0)
    eye_cols = lax.broadcasted_iota(jnp.int32, (half, CHUNK), 1)

    def make_step(y, z, arrivals):
        for n in range(chunks):
            moment = product(y[mine, :], z, arrivals, n)
            eye = jnp.where(eye_rows == eye_cols + n * CHUNK, 3.0, 0.0)
            step[:, cols(n)] = ((eye - moment) * 0.5).astype(bf16)

    y, z, z_in = full.at[2], z1, None
    y_in = advance(z1.at[mine], y0, None, y, 0)
    slot, ex = 3, 1
    for _ in range(ITERS - 2):
        make_step(y, z, z_in)
        z_next, y_next = full.at[slot], full.at[slot + 1]
        z_in_next = advance(step, z, None, z_next, ex)
        y_in = advance(step, y, y_in, y_next, ex + 1)
        y, z, z_in = y_next, z_next, z_in_next
        slot, ex = slot + 2, ex + 2
    make_step(y, z, z_in)

    for n in range(chunks):
        z1[0:half, cols(n)] = product(step[...], z, None, n).astype(bf16)

    def local_rows(r):
        return pl.ds(pl.multiple_of(r * rows, rows), rows)

    invs = []
    for k in range(1, reps):
        p = target(k)
        copy = remote(
            z1.at[local_rows(p)], inv_ref.at[rep], inv_send.at[k], inv_recv.at[k], p, blk
        )
        copy.start()
        invs.append(copy)

    my_cols = pl.ds(pl.multiple_of(blk * half, LANES), half)
    for n in range(chunks):
        out = product(step[...], y, y_in, n)
        last_root[cols(n), :] = out.T.astype(bf16)
    roots = []
    for k in list(range(1, reps)) + [0]:
        for flip in range(2):
            if k == 0 and flip == 0:
                continue
            r = target(k) if k else rep
            b = blk + flip - 2 * blk * flip
            copy = remote(
                last_root.at[block_rows(b, r)], root_ref.at[rep, :, my_cols],
                root_send.at[k, flip], root_recv.at[k, flip], r, b,
            )
            copy.start()
            roots.append(copy)
    inv_ref[rep] = z1[local_rows(rep), :]
    root_ref[rep, :, my_cols] = last_root[block_rows(blk, rep), :]

    for k in range(1, reps):
        each(pieces(k, rep, 1 - side), functools.partial(wait_in, k))
    for copy in pending:
        copy.wait_send()
    for copy in invs + roots:
        copy.wait()


def fused(mesh, factors, damping):
    facs, rows, order = factors.shape
    reps = mesh.shape["rep"]
    members = 2 * reps
    half = rows * reps
    chunks = order // CHUNK
    dma = pltpu.SemaphoreType.DMA
    vmem = pl.BlockSpec(memory_space=pltpu.VMEM)
    exchanges = 2 * ITERS - 3
    root, inv, norm = pl.pallas_call(
        functools.partial(kernel, reps),
        out_shape=(
            jax.ShapeDtypeStruct(factors.shape, jnp.bfloat16),
            jax.ShapeDtypeStruct(factors.shape, jnp.bfloat16),
            jax.ShapeDtypeStruct((facs, LANES), jnp.float32),
        ),
        in_specs=[
            pl.BlockSpec(memory_space=pl.ANY),
            pl.BlockSpec(memory_space=pltpu.SMEM),
        ],
        out_specs=(vmem, vmem, vmem),
        scratch_shapes=[
            pltpu.VMEM(factors.shape, jnp.float32),
            pltpu.VMEM((members, facs, LANES), jnp.float32),
            pltpu.VMEM((facs, LANES), jnp.float32),
            pltpu.VMEM(factors.shape, jnp.bfloat16),
            pltpu.VMEM((2 * ITERS - 1, order, order), jnp.bfloat16),
            pltpu.VMEM((half, order), jnp.bfloat16),
            pltpu.VMEM((order, half), jnp.bfloat16),
            dma((facs,)),
            dma((members,)), dma((members,)),
            dma((reps, 2)), dma((reps, 2)),
            dma((reps, 2)), dma((reps, 2)),
            dma((exchanges, chunks)), dma((exchanges, chunks)),
            dma((reps, 2)), dma((reps, 2)),
            dma((reps,)), dma((reps,)),
        ],
        compiler_params=pltpu.CompilerParams(
            collective_id=0, has_side_effects=True, vmem_limit_bytes=60 * 2**20
        ),
    )(factors, damping)
    root_scale = jnp.sqrt(norm[:, :1])[:, :, None]
    return root.astype(jnp.float32) * root_scale, inv.astype(jnp.float32) / root_scale


def plain(factors, damping):
    fac_grp, row_count, order_full = factors.shape
    rep_count = lax.axis_size("rep")
    fac_rep = fac_grp // rep_count
    blk_rows = row_count * rep_count
    blk_idx = lax.axis_index("blk")
    rep_idx = lax.axis_index("rep")
    row_ids = blk_idx * blk_rows + rep_idx * row_count + lax.iota(jnp.int32, row_count)
    col_ids = lax.iota(jnp.int32, order_full)
    eye_block = (row_ids[:, None] == col_ids[None, :]).astype(jnp.float32)
    damped = factors + damping[:, None, None] * eye_block[None, :, :]
    factor_norms = jnp.sqrt(lax.psum(jnp.sum(damped * damped, axis=(1, 2)), ("rep", "blk")))
    own_rows = lax.all_to_all(damped, "rep", split_axis=0, concat_axis=1, tiled=True)
    own_norms = lax.dynamic_slice_in_dim(factor_norms, rep_idx * fac_rep, fac_rep)
    iterate = (own_rows / own_norms[:, None, None]).astype(jnp.bfloat16)
    iter_rows = blk_idx * blk_rows + lax.iota(jnp.int32, blk_rows)
    eye_rows = (iter_rows[:, None] == col_ids[None, :]).astype(jnp.float32)
    inverse = eye_rows[None, :, :].astype(jnp.bfloat16)
    for _ in range(ITERS):
        whole_iter = lax.all_gather(iterate, "blk", axis=1, tiled=True)
        whole_inv = lax.all_gather(inverse, "blk", axis=1, tiled=True)
        eye_full = jnp.eye(order_full, dtype=jnp.float32)
        moment = jnp.einsum(
            "fik,fkj->fij", whole_inv, whole_iter, preferred_element_type=jnp.float32
        )
        step = ((3.0 * eye_full[None, :, :] - moment) * 0.5).astype(jnp.bfloat16)
        step_rows = lax.dynamic_slice_in_dim(step, blk_idx * blk_rows, blk_rows, 1)
        new_iterate = jnp.einsum("fik,fkj->fij", iterate, step, preferred_element_type=jnp.float32)
        new_inverse = jnp.einsum(
            "fik,fkj->fij", step_rows, whole_inv, preferred_element_type=jnp.float32
        )
        iterate = new_iterate.astype(jnp.bfloat16)
        inverse = new_inverse.astype(jnp.bfloat16)
    root = lax.all_to_all(iterate, "rep", split_axis=1, concat_axis=0, tiled=True)
    inv = lax.all_to_all(inverse, "rep", split_axis=1, concat_axis=0, tiled=True)
    root_scale = jnp.sqrt(factor_norms)[:, None, None]
    return root.astype(jnp.float32) * root_scale, inv.astype(jnp.float32) / root_scale


def solution(mesh):
    def per_device(factors, damping):
        facs, rows, order = factors.shape
        if (
            facs == mesh.shape["rep"]
            and mesh.shape["blk"] == 2
            and rows % 16 == 0
            and facs % 2 == 0
            and (rows * facs) % LANES == 0
            and order % CHUNK == 0
        ):
            return fused(mesh, factors, damping)
        return plain(factors, damping)

    return jax.shard_map(
        per_device,
        mesh=mesh,
        in_specs=(P("grp", ("blk", "rep"), None), P("grp")),
        out_specs=(P("grp", ("blk", "rep"), None), P("grp", ("blk", "rep"), None)),
        check_vma=False,
    )
```

profile of v0, /device:TPU:0, one launch (start us, length us, event | category | flops | bytes accessed | tf_op | source)
XLA Modules:
  0.0 154.4 jit_solution(11749190187257543410)
XLA Ops:
  0.6 147.5 %shard_map.41 = (bf16[8,80,1280]{2,1,0:T(8,128)(2,1)}, bf16[8,80,1280]{2,1,0:T(8,128)(2,1)}, f32[8,128]{1,0:T(8,128)}) custom-call(f32[8,80,1280]{2,1,0:T(8,128)} %fac_hbm.1, f32[8]{0:T(128)} %damp_ref.1), custom_call_target="tpu_custom_call" | custom-call | tf_op jit(solution)/shard_map/pallas_call | solution.py:311
  148.2 0.8 sqrt_reduce_fusion
  149.0 5.5 %convert_divide_fusion = (f32[8,80,1280]{2,1,0:T(8,128)}, f32[8,80,1280]{2,1,0:T(8,128)}) fusion(bf16[8,80,1280]{2,1,0:T(8,128)(2,1)} %get-tuple-element.7, f32[8]{0:T(128)S(1)} %sqrt_reduce_fusion, bf16[8,80,1280]{2,1,0:T(8,128)(2,1)} %get-tuple-element.5), kind=kLoop, calls=%fused_computation | loop fusion | flops 3276800 | bytes 9830432 | tf_op jit(solution)/shard_map/div | solution.py:344
where the time goes:
time: 155 us; the launch traced here: 154 us
  Pallas kernels  148 us (95%)
  other arithmetic  5.48 us (4%)
    pallas_call x1, Pallas kernels, fused(): pl.pallas_call(functools.partial(kernel, reps), out_shape=(jax.ShapeDtype...  148 us
    div x1, other arithmetic, fused(): inv.astype(jnp.float32) / root_scale  5.48 us

commit v1 on v0

v1 whole, which is shorter than its diff:
```python
import functools

import jax
import jax.numpy as jnp
from jax import lax
from jax.experimental import pallas as pl
from jax.experimental.pallas import tpu as pltpu
from jax.sharding import PartitionSpec as P

ITERS = 4
LANES = 128
CHUNK = 256
MESH = pl.DeviceIdType.MESH


def kernel(
    reps, fac_hbm, damp_ref,
    root_ref, inv_ref, norm_ref,
    fac, part, scale, send_buf, full, z1, step, near_y, last_root, last_inv,
    load_sem, sum_send, sum_recv, in_send, in_recv, fwd_send, fwd_recv,
    ex_send, ex_recv, root_send, root_recv, inv_send, inv_recv,
):
    grp = lax.axis_index("grp")
    rep = lax.axis_index("rep")
    blk = lax.axis_index("blk")
    facs, rows, order = fac.shape
    half = rows * reps
    members = 2 * reps
    rank = blk * reps + rep
    chunks = order // CHUNK
    f32, bf16 = jnp.float32, jnp.bfloat16

    side_reps = reps // 2
    side = rep // side_reps
    place = lax.rem(rep, side_reps)
    slots = facs // side_reps
    held = full.shape[0] // slots

    def factor_of(j, r):
        return j * side_reps + lax.rem(r, side_reps)

    def remote(src, dst, send, recv, r, b):
        return pltpu.make_async_remote_copy(
            src_ref=src, dst_ref=dst, send_sem=send, recv_sem=recv,
            device_id=(grp, r, b), device_id_type=MESH,
        )

    def member(j):
        q = lax.rem(rank + j, members)
        return lax.rem(q, reps), q // reps

    loads = [
        pltpu.make_async_copy(fac_hbm.at[f], fac.at[f], load_sem.at[f]) for f in range(facs)
    ]
    for load in loads:
        load.start()
    barrier = pltpu.get_barrier_semaphore()
    for j in range(1, members):
        r, b = member(j)
        pl.semaphore_signal(barrier, inc=1, device_id=(grp, r, b), device_id_type=MESH)

    row_ids = rank * rows + lax.broadcasted_iota(jnp.int32, (rows, order), 0)
    diag = row_ids == lax.broadcasted_iota(jnp.int32, (rows, order), 1)

    def damped(f):
        return fac[f] + jnp.where(diag, damp_ref[f], 0.0)

    for f in range(facs):
        loads[f].wait()
        x = damped(f)
        col = jnp.sum(x * x, axis=0, keepdims=True)
        acc = col[:, :LANES]
        for c in range(1, order // LANES):
            acc = acc + col[:, c * LANES : (c + 1) * LANES]
        part[pl.ds(rank, 1), f : f + 1, :] = acc[None]
    pl.semaphore_wait(barrier, members - 1)

    sums = []
    for j in range(1, members):
        r, b = member(j)
        copy = remote(part.at[rank], part.at[rank], sum_send.at[j], sum_recv.at[j], r, b)
        copy.start()
        sums.append(copy)
    for copy in sums:
        copy.wait()
    total = part[0]
    for q in range(1, members):
        total = total + part[q]
    norm = jnp.sqrt(jnp.sum(total, axis=1, keepdims=True))
    norm_ref[...] = jnp.broadcast_to(norm, norm_ref.shape)
    scale[...] = jnp.broadcast_to(1.0 / norm, scale.shape)

    def block_rows(b, r):
        return pl.ds(pl.multiple_of((b * reps + r) * rows, rows), rows)

    wide = -(-(half // 2) // LANES) * LANES
    narrow = half - wide

    def target(k):
        if k <= side_reps:
            return (1 - side) * side_reps + lax.rem(rep + k, side_reps)
        return side * side_reps + lax.rem(rep + k, side_reps)

    def source(k):
        if k == 0:
            return rep
        back = lax.rem(rep - k + reps, side_reps)
        if k <= side_reps:
            return (1 - side) * side_reps + back
        return side * side_reps + back

    tiles = half // LANES
    widths = sorted({tiles - (r * rows) // LANES for r in range(side_reps, reps)})

    def width_of(r, owner_side):
        mirrored = r + owner_side * (reps - 1 - 2 * r)
        return tiles - (mirrored * rows) // LANES

    def pieces(k, src, owner_side):
        if k == 0 or k > side_reps:
            return [(None, [pl.ds(0, order)])]
        options = []
        for w in widths:
            first = (1 - owner_side) * (half - w * LANES)
            options.append((
                width_of(src, owner_side) == w,
                [pl.ds(pl.multiple_of(h * half + first, LANES), w * LANES) for h in range(2)],
            ))
        return options

    def each(options, act):
        for condition, columns in options:
            if condition is None:
                act(columns)
            else:
                pl.when(condition)(functools.partial(act, columns))

    own_rows = block_rows(blk, rep)
    far_ks = list(range(1, side_reps + 1))
    near_ks = list(range(side_reps + 1, reps))

    def start_of(j):
        return full.at[j * held]

    def in_copy(j, k, i, c):
        p = target(k)
        return remote(
            send_buf.at[factor_of(j, p), :, c], start_of(j).at[own_rows, c],
            in_send.at[j, k, i], in_recv.at[j, k, i], p, blk,
        )

    def send_in(j, k, columns):
        for i, c in enumerate(columns):
            in_copy(j, k, i, c).start()

    def wait_in(j, k, columns):
        for i, c in enumerate(columns):
            in_copy(j, k, i, c).wait_send()

    for j in range(slots):
        for k in far_ks:
            p = factor_of(j, target(k))
            rounded = (damped(p) * scale[pl.ds(p, 1), 0:1]).astype(bf16)
            send_buf[p] = rounded
            if k == side_reps:
                start_of(j)[own_rows, :] = rounded
            each(pieces(k, rep, 1 - side), functools.partial(send_in, j, k))
        for k in near_ks:
            each(pieces(k, rep, 1 - side), functools.partial(send_in, j, k))

    def forward_copy(j, k, i, c):
        at = block_rows(blk, source(k))
        y0 = start_of(j)
        return remote(
            y0.at[at, c], y0.at[at, c], fwd_send.at[j, k, i], fwd_recv.at[j, k, i],
            rep, 1 - blk,
        )

    def forward(j, k, columns):
        for i, c in enumerate(columns):
            if k:
                in_copy(j, k, i, c).wait_recv()
            forward_copy(j, k, i, c).start()

    def wait_forward(j, k, columns):
        for i, c in enumerate(columns):
            forward_copy(j, k, i, c).wait()

    def forward_all(j):
        for k in [0] + near_ks + far_ks:
            each(pieces(k, source(k), side), functools.partial(forward, j, k))

    far = half // 2
    miss = half - min(widths) * LANES

    def fill(t, old, row0, col0, mirrored):
        shape = (far, miss)
        r = (row0 + lax.broadcasted_iota(jnp.int32, shape, 0)) // rows
        c = (col0 + lax.broadcasted_iota(jnp.int32, shape, 1)) // LANES
        if mirrored:
            gone = c >= tiles - ((reps - 1 - r) * rows) // LANES
        else:
            gone = c < (r * rows) // LANES
        return jnp.where(gone, t, old.astype(f32)).astype(bf16)

    mine = pl.ds(pl.multiple_of(blk * half, half), half)
    my_cols = pl.ds(pl.multiple_of(blk * half, LANES), half)
    near_rows = pl.ds(pl.multiple_of(side * far, far), far)
    eye_rows = blk * half + lax.broadcasted_iota(jnp.int32, (half, CHUNK), 0)
    eye_cols = lax.broadcasted_iota(jnp.int32, (half, CHUNK), 1)

    def cols(n):
        return slice(n * CHUNK, (n + 1) * CHUNK)

    def inv_copy(j, k):
        p = target(k)
        at = pl.ds(pl.multiple_of(lax.rem(p, side_reps) * rows, rows), rows)
        return remote(
            last_inv.at[j, at], inv_ref.at[factor_of(j, rep)],
            inv_send.at[j, k], inv_recv.at[j, k], p, blk,
        )

    def root_rows(b, r):
        first = b * wide + side * (far - narrow) + lax.rem(r, side_reps) * rows
        return pl.ds(pl.multiple_of(first, 16), rows)

    def root_copy(j, k, flip):
        r = target(k) if k else rep
        b = blk + flip - 2 * blk * flip
        return remote(
            last_root.at[j, root_rows(b, r)], root_ref.at[factor_of(j, rep), :, my_cols],
            root_send.at[j, k, flip], root_recv.at[j, k, flip], r, b,
        )

    root_ks = [(k, flip) for k in near_ks for flip in range(2)] + [(0, 1)]

    def iterate(j, carry):
        for k in range(reps):
            each(pieces(k, source(k), side), functools.partial(wait_forward, j, k))
        y0 = start_of(j)

        @pl.when(side == 0)
        def _():
            for hi in range(2):
                for hj in range(2):
                    t = y0[hj * half : hj * half + miss, hi * half + narrow : (hi + 1) * half]
                    at = (
                        slice(hi * half + far, (hi + 1) * half),
                        slice(hj * half, hj * half + miss),
                    )
                    t = t.astype(f32).T[far - narrow :, :]
                    y0[at] = fill(t, y0[at], far, 0, False)

        @pl.when(side == 1)
        def _():
            for hi in range(2):
                for hj in range(2):
                    t = y0[(hj + 1) * half - miss : (hj + 1) * half, hi * half : hi * half + wide]
                    at = (
                        slice(hi * half, hi * half + far),
                        slice((hj + 1) * half - miss, (hj + 1) * half),
                    )
                    t = t.astype(f32).T[:far, :]
                    y0[at] = fill(t, y0[at], 0, half - miss, True)

        for q in range(members):
            at = slice(q * rows, (q + 1) * rows)
            ids = q * rows + lax.broadcasted_iota(jnp.int32, (rows, order), 0)
            eye = ids == lax.broadcasted_iota(jnp.int32, (rows, order), 1)
            z1[at, :] = ((jnp.where(eye, 3.0, 0.0) - y0[at, :].astype(f32)) * 0.5).astype(bf16)

        pending = []

        def share(dst, ex, n):
            view = dst.at[mine, pl.ds(n * CHUNK, CHUNK)]
            copy = remote(view, view, ex_send.at[j, ex, n], ex_recv.at[j, ex, n], rep, 1 - blk)
            copy.start()
            pending.append(copy)
            return copy

        def product(lhs, rhs, arrivals, n):
            if arrivals is not None:
                arrivals[n].wait_recv()
            return jnp.dot(lhs, rhs[:, cols(n)], preferred_element_type=f32)

        def advance(lhs, rhs, arrivals, dst, ex):
            shared = []
            for n in range(chunks):
                dst[mine, cols(n)] = product(lhs[...], rhs, arrivals, n).astype(bf16)
                shared.append(share(dst, ex, n))
            return shared

        def make_step(y, z, arrivals):
            for n in range(chunks):
                moment = product(y[mine, :], z, arrivals, n)
                eye = jnp.where(eye_rows == eye_cols + n * CHUNK, 3.0, 0.0)
                step[:, cols(n)] = ((eye - moment) * 0.5).astype(bf16)

        base = j * held
        y, z, z_in = full.at[base + 1], z1, None
        y_in = advance(z1.at[mine], y0, None, y, 0)
        slot, ex = 2, 1
        for _ in range(ITERS - 2):
            make_step(y, z, z_in)
            z_next, y_next = full.at[base + slot], full.at[base + slot + 1]
            z_in_next = advance(step, z, None, z_next, ex)
            y_in = advance(step, y, y_in, y_next, ex + 1)
            y, z, z_in = y_next, z_next, z_in_next
            slot, ex = slot + 2, ex + 2
        make_step(y, z, z_in)

        for n in range(chunks):
            last_inv[j, :, cols(n)] = product(step[near_rows, :], z, None, n).astype(bf16)
        for k in near_ks:
            inv_copy(j, k).start()

        @pl.when(j + 1 < slots)
        def _():
            forward_all(j + 1)

        for copy in y_in:
            copy.wait_recv()
        for h in range(2):
            at = pl.ds(pl.multiple_of(h * half + side * narrow, LANES), wide)
            near_y[:, h * wide : (h + 1) * wide] = y[:, at]
        for n in range(2 * wide // CHUNK):
            out = product(step[...], near_y, None, n)
            last_root[j, cols(n), :] = out.T.astype(bf16)
        for k, flip in root_ks:
            root_copy(j, k, flip).start()
        own = factor_of(j, rep)
        local = pl.ds(pl.multiple_of(place * rows, rows), rows)
        inv_ref[own] = last_inv[j, local, :]
        root_ref[own, :, my_cols] = last_root[j, root_rows(blk, rep), :]
        for copy in pending:
            copy.wait_send()
        return carry

    forward_all(0)
    lax.fori_loop(0, slots, iterate, 0)

    for j in range(slots):
        for k in range(1, reps):
            each(pieces(k, rep, 1 - side), functools.partial(wait_in, j, k))
    for j in range(slots):
        for k in near_ks:
            inv_copy(j, k).wait()
        for k, flip in root_ks:
            root_copy(j, k, flip).wait()


def fused(mesh, factors, damping):
    facs, rows, order = factors.shape
    reps = mesh.shape["rep"]
    members = 2 * reps
    half = rows * reps
    chunks = order // CHUNK
    slots = 2
    wide = -(-(half // 2) // LANES) * LANES
    dma = pltpu.SemaphoreType.DMA
    vmem = pl.BlockSpec(memory_space=pltpu.VMEM)
    exchanges = 2 * ITERS - 3
    bf16 = jnp.bfloat16
    root, inv, norm = pl.pallas_call(
        functools.partial(kernel, reps),
        out_shape=(
            jax.ShapeDtypeStruct(factors.shape, bf16),
            jax.ShapeDtypeStruct(factors.shape, bf16),
            jax.ShapeDtypeStruct((facs, LANES), jnp.float32),
        ),
        in_specs=[
            pl.BlockSpec(memory_space=pl.ANY),
            pl.BlockSpec(memory_space=pltpu.SMEM),
        ],
        out_specs=(vmem, vmem, vmem),
        scratch_shapes=[
            pltpu.VMEM(factors.shape, jnp.float32),
            pltpu.VMEM((members, facs, LANES), jnp.float32),
            pltpu.VMEM((facs, LANES), jnp.float32),
            pltpu.VMEM(factors.shape, bf16),
            pltpu.VMEM((slots * (2 * ITERS - 2), order, order), bf16),
            pltpu.VMEM((order, order), bf16),
            pltpu.VMEM((half, order), bf16),
            pltpu.VMEM((order, 2 * wide), bf16),
            pltpu.VMEM((slots, 2 * wide, half), bf16),
            pltpu.VMEM((slots, half // 2, order), bf16),
            dma((facs,)),
            dma((members,)), dma((members,)),
            dma((slots, reps, 2)), dma((slots, reps, 2)),
            dma((slots, reps, 2)), dma((slots, reps, 2)),
            dma((slots, exchanges, chunks)), dma((slots, exchanges, chunks)),
            dma((slots, reps, 2)), dma((slots, reps, 2)),
            dma((slots, reps)), dma((slots, reps)),
        ],
        compiler_params=pltpu.CompilerParams(
            collective_id=0, has_side_effects=True, vmem_limit_bytes=63 * 2**20
        ),
    )(factors, damping)
    root_scale = jnp.sqrt(norm[:, :1])[:, :, None]
    return root.astype(jnp.float32) * root_scale, inv.astype(jnp.float32) / root_scale


def plain(factors, damping):
    fac_grp, row_count, order_full = factors.shape
    rep_count = lax.axis_size("rep")
    fac_rep = fac_grp // rep_count
    blk_rows = row_count * rep_count
    blk_idx = lax.axis_index("blk")
    rep_idx = lax.axis_index("rep")
    row_ids = blk_idx * blk_rows + rep_idx * row_count + lax.iota(jnp.int32, row_count)
    col_ids = lax.iota(jnp.int32, order_full)
    eye_block = (row_ids[:, None] == col_ids[None, :]).astype(jnp.float32)
    damped = factors + damping[:, None, None] * eye_block[None, :, :]
    factor_norms = jnp.sqrt(lax.psum(jnp.sum(damped * damped, axis=(1, 2)), ("rep", "blk")))
    own_rows = lax.all_to_all(damped, "rep", split_axis=0, concat_axis=1, tiled=True)
    own_norms = lax.dynamic_slice_in_dim(factor_norms, rep_idx * fac_rep, fac_rep)
    iterate = (own_rows / own_norms[:, None, None]).astype(jnp.bfloat16)
    iter_rows = blk_idx * blk_rows + lax.iota(jnp.int32, blk_rows)
    eye_rows = (iter_rows[:, None] == col_ids[None, :]).astype(jnp.float32)
    inverse = eye_rows[None, :, :].astype(jnp.bfloat16)
    for _ in range(ITERS):
        whole_iter = lax.all_gather(iterate, "blk", axis=1, tiled=True)
        whole_inv = lax.all_gather(inverse, "blk", axis=1, tiled=True)
        eye_full = jnp.eye(order_full, dtype=jnp.float32)
        moment = jnp.einsum(
            "fik,fkj->fij", whole_inv, whole_iter, preferred_element_type=jnp.float32
        )
        step = ((3.0 * eye_full[None, :, :] - moment) * 0.5).astype(jnp.bfloat16)
        step_rows = lax.dynamic_slice_in_dim(step, blk_idx * blk_rows, blk_rows, 1)
        new_iterate = jnp.einsum("fik,fkj->fij", iterate, step, preferred_element_type=jnp.float32)
        new_inverse = jnp.einsum(
            "fik,fkj->fij", step_rows, whole_inv, preferred_element_type=jnp.float32
        )
        iterate = new_iterate.astype(jnp.bfloat16)
        inverse = new_inverse.astype(jnp.bfloat16)
    root = lax.all_to_all(iterate, "rep", split_axis=1, concat_axis=0, tiled=True)
    inv = lax.all_to_all(inverse, "rep", split_axis=1, concat_axis=0, tiled=True)
    root_scale = jnp.sqrt(factor_norms)[:, None, None]
    return root.astype(jnp.float32) * root_scale, inv.astype(jnp.float32) / root_scale


def solution(mesh):
    def per_device(factors, damping):
        facs, rows, order = factors.shape
        if (
            facs == mesh.shape["rep"]
            and mesh.shape["blk"] == 2
            and rows % 16 == 0
            and facs % 2 == 0
            and (rows * facs) % LANES == 0
            and 2 * -(-(rows * facs // 2) // LANES) * LANES % CHUNK == 0
            and order % CHUNK == 0
        ):
            return fused(mesh, factors, damping)
        return plain(factors, damping)

    return jax.shard_map(
        per_device,
        mesh=mesh,
        in_specs=(P("grp", ("blk", "rep"), None), P("grp")),
        out_specs=(P("grp", ("blk", "rep"), None), P("grp", ("blk", "rep"), None)),
        check_vma=False,
    )
```

time: 155 us -> 153 us (0.987)
  Pallas kernels: 148 us -> 146 us
    pallas_call x1, Pallas kernels: 148 us -> 146 us  [fused(): pl.pallas_call(functools.partial(kernel, reps), out_shape=(jax.ShapeDtype...]
where the time goes in v1:
time: 153 us; the launch traced here: 152 us
  Pallas kernels  146 us (95%)
  other arithmetic  5.48 us (4%)
    pallas_call x1, Pallas kernels, fused(): pl.pallas_call(functools.partial(kernel, reps), out_shape=(jax.ShapeDtype...  146 us
    div x1, other arithmetic, fused(): inv.astype(jnp.float32) / root_scale  5.48 us

profile of v1, /device:TPU:0, one launch (start us, length us, event | category | flops | bytes accessed | tf_op | source)
XLA Modules:
  0.0 152.4 jit_solution(9152094211711575064)
XLA Ops:
  0.6 145.5 %shard_map.41 = (bf16[8,80,1280]{2,1,0:T(8,128)(2,1)}, bf16[8,80,1280]{2,1,0:T(8,128)(2,1)}, f32[8,128]{1,0:T(8,128)}) custom-call(f32[8,80,1280]{2,1,0:T(8,128)} %fac_hbm.1, f32[8]{0:T(128)} %damp_ref.1), custom_call_target="tpu_custom_call" | custom-call | tf_op jit(solution)/shard_map/pallas_call | solution.py:364
  146.2 0.8 sqrt_reduce_fusion
  147.0 5.5 %convert_divide_fusion = (f32[8,80,1280]{2,1,0:T(8,128)}, f32[8,80,1280]{2,1,0:T(8,128)}) fusion(bf16[8,80,1280]{2,1,0:T(8,128)(2,1)} %get-tuple-element.7, f32[8]{0:T(128)S(1)} %sqrt_reduce_fusion, bf16[8,80,1280]{2,1,0:T(8,128)(2,1)} %get-tuple-element.5), kind=kLoop, calls=%fused_computation | loop fusion | flops 3276800 | bytes 9830432 | tf_op jit(solution)/shard_map/div | solution.py:400

commit v2 on v1

--- a/solution.py
+++ b/solution.py
@@ -16,7 +16,7 @@
 def kernel(
     reps, fac_hbm, damp_ref,
     root_ref, inv_ref, norm_ref,
-    fac, part, scale, send_buf, full, z1, step, near_y, last_root, last_inv,
+    fac, part, scale, send_buf, start, held, z1, step, near_y, last_root, last_inv,
     load_sem, sum_send, sum_recv, in_send, in_recv, fwd_send, fwd_recv,
     ex_send, ex_recv, root_send, root_recv, inv_send, inv_recv,
 ):
@@ -34,7 +34,6 @@
     side = rep // side_reps
     place = lax.rem(rep, side_reps)
     slots = facs // side_reps
-    held = full.shape[0] // slots
 
     def factor_of(j, r):
         return j * side_reps + lax.rem(r, side_reps)
@@ -140,7 +139,7 @@
     near_ks = list(range(side_reps + 1, reps))
 
     def start_of(j):
-        return full.at[j * held]
+        return start.at[j]
 
     def in_copy(j, k, i, c):
         p = target(k)
@@ -208,6 +207,8 @@
     near_rows = pl.ds(pl.multiple_of(side * far, far), far)
     eye_rows = blk * half + lax.broadcasted_iota(jnp.int32, (half, CHUNK), 0)
     eye_cols = lax.broadcasted_iota(jnp.int32, (half, CHUNK), 1)
+
+    parts = [(0, (chunks + 1) // 2), ((chunks + 1) // 2, chunks)]
 
     def cols(n):
         return slice(n * CHUNK, (n + 1) * CHUNK)
@@ -271,46 +272,53 @@
 
         pending = []
 
-        def share(dst, ex, n):
-            view = dst.at[mine, pl.ds(n * CHUNK, CHUNK)]
-            copy = remote(view, view, ex_send.at[j, ex, n], ex_recv.at[j, ex, n], rep, 1 - blk)
+        def share(dst, ex, part):
+            first, last = parts[part]
+            view = dst.at[mine, pl.ds(first * CHUNK, (last - first) * CHUNK)]
+            copy = remote(
+                view, view, ex_send.at[j, ex, part], ex_recv.at[j, ex, part], rep, 1 - blk
+            )
             copy.start()
             pending.append(copy)
             return copy
 
-        def product(lhs, rhs, arrivals, n):
-            if arrivals is not None:
-                arrivals[n].wait_recv()
+        def settle(arrivals):
+            for copy in arrivals:
+                copy.wait_recv()
+
+        def product(lhs, rhs, n):
             return jnp.dot(lhs, rhs[:, cols(n)], preferred_element_type=f32)
 
         def advance(lhs, rhs, arrivals, dst, ex):
+            settle(arrivals)
             shared = []
+            for part, (first, last) in enumerate(parts):
+                for n in range(first, last):
+                    dst[mine, cols(n)] = product(lhs[...], rhs, n).astype(bf16)
+                shared.append(share(dst, ex, part))
+            return shared
+
+        def make_step(y, z, arrivals):
+            settle(arrivals)
             for n in range(chunks):
-                dst[mine, cols(n)] = product(lhs[...], rhs, arrivals, n).astype(bf16)
-                shared.append(share(dst, ex, n))
-            return shared
-
-        def make_step(y, z, arrivals):
-            for n in range(chunks):
-                moment = product(y[mine, :], z, arrivals, n)
+                moment = product(y[mine, :], z, n)
                 eye = jnp.where(eye_rows == eye_cols + n * CHUNK, 3.0, 0.0)
                 step[:, cols(n)] = ((eye - moment) * 0.5).astype(bf16)
 
-        base = j * held
-        y, z, z_in = full.at[base + 1], z1, None
-        y_in = advance(z1.at[mine], y0, None, y, 0)
-        slot, ex = 2, 1
+        y, z, z_in = held[0].at[j], z1, []
+        y_in = advance(z1.at[mine], y0, [], y, 0)
+        ex = 1
         for _ in range(ITERS - 2):
             make_step(y, z, z_in)
-            z_next, y_next = full.at[base + slot], full.at[base + slot + 1]
-            z_in_next = advance(step, z, None, z_next, ex)
+            z_next, y_next = held[ex].at[j], held[ex + 1].at[j]
+            z_in_next = advance(step, z, [], z_next, ex)
             y_in = advance(step, y, y_in, y_next, ex + 1)
             y, z, z_in = y_next, z_next, z_in_next
-            slot, ex = slot + 2, ex + 2
+            ex = ex + 2
         make_step(y, z, z_in)
 
         for n in range(chunks):
-            last_inv[j, :, cols(n)] = product(step[near_rows, :], z, None, n).astype(bf16)
+            last_inv[j, :, cols(n)] = product(step[near_rows, :], z, n).astype(bf16)
         for k in near_ks:
             inv_copy(j, k).start()
 
@@ -318,13 +326,12 @@
         def _():
             forward_all(j + 1)
 
-        for copy in y_in:
-            copy.wait_recv()
+        settle(y_in)
         for h in range(2):
             at = pl.ds(pl.multiple_of(h * half + side * narrow, LANES), wide)
             near_y[:, h * wide : (h + 1) * wide] = y[:, at]
         for n in range(2 * wide // CHUNK):
-            out = product(step[...], near_y, None, n)
+            out = product(step[...], near_y, n)
             last_root[j, cols(n), :] = out.T.astype(bf16)
         for k, flip in root_ks:
             root_copy(j, k, flip).start()
@@ -354,7 +361,6 @@
     reps = mesh.shape["rep"]
     members = 2 * reps
     half = rows * reps
-    chunks = order // CHUNK
     slots = 2
     wide = -(-(half // 2) // LANES) * LANES
     dma = pltpu.SemaphoreType.DMA
@@ -378,7 +384,8 @@
             pltpu.VMEM((members, facs, LANES), jnp.float32),
             pltpu.VMEM((facs, LANES), jnp.float32),
             pltpu.VMEM(factors.shape, bf16),
-            pltpu.VMEM((slots * (2 * ITERS - 2), order, order), bf16),
+            pltpu.VMEM((slots, order, order), bf16),
+            [pltpu.VMEM((slots, order, order), bf16) for _ in range(exchanges)],
             pltpu.VMEM((order, order), bf16),
             pltpu.VMEM((half, order), bf16),
             pltpu.VMEM((order, 2 * wide), bf16),
@@ -388,7 +395,7 @@
             dma((members,)), dma((members,)),
             dma((slots, reps, 2)), dma((slots, reps, 2)),
             dma((slots, reps, 2)), dma((slots, reps, 2)),
-            dma((slots, exchanges, chunks)), dma((slots, exchanges, chunks)),
+            dma((slots, exchanges, 2)), dma((slots, exchanges, 2)),
             dma((slots, reps, 2)), dma((slots, reps, 2)),
             dma((slots, reps)), dma((slots, reps)),
         ],

time: 153 us -> 119 us (0.78)
  Pallas kernels: 146 us -> 112 us
    pallas_call x1, Pallas kernels: 146 us -> 112 us  [fused(): pl.pallas_call(functools.partial(kernel, reps), out_shape=(jax.ShapeDtype...]
where the time goes in v2:
time: 119 us
  Pallas kernels  112 us (94%)
  other arithmetic  5.48 us (5%)
    pallas_call x1, Pallas kernels, fused(): pl.pallas_call(functools.partial(kernel, reps), out_shape=(jax.ShapeDtype...  112 us
    div x1, other arithmetic, fused(): inv.astype(jnp.float32) / root_scale  5.48 us

profile of v2, /device:TPU:0, one launch (start us, length us, event | category | flops | bytes accessed | tf_op | source)
XLA Modules:
  0.0 119.1 jit_solution(12402727601976863137)
XLA Ops:
  0.6 112.1 %shard_map.41 = (bf16[8,80,1280]{2,1,0:T(8,128)(2,1)}, bf16[8,80,1280]{2,1,0:T(8,128)(2,1)}, f32[8,128]{1,0:T(8,128)}) custom-call(f32[8,80,1280]{2,1,0:T(8,128)} %fac_hbm.1, f32[8]{0:T(128)} %damp_ref.1), custom_call_target="tpu_custom_call" | custom-call | tf_op jit(solution)/shard_map/pallas_call | solution.py:370
  112.8 0.8 sqrt_reduce_fusion
  113.6 5.5 %convert_divide_fusion = (f32[8,80,1280]{2,1,0:T(8,128)}, f32[8,80,1280]{2,1,0:T(8,128)}) fusion(bf16[8,80,1280]{2,1,0:T(8,128)(2,1)} %get-tuple-element.7, f32[8]{0:T(128)S(1)} %sqrt_reduce_fusion, bf16[8,80,1280]{2,1,0:T(8,128)(2,1)} %get-tuple-element.5), kind=kLoop, calls=%fused_computation | loop fusion | flops 3276800 | bytes 9830432 | tf_op jit(solution)/shard_map/div | solution.py:407

commit v3 on v2

--- a/solution.py
+++ b/solution.py
@@ -156,16 +156,24 @@
         for i, c in enumerate(columns):
             in_copy(j, k, i, c).wait_send()
 
-    for j in range(slots):
+    def round_rows(j, k):
+        p = factor_of(j, target(k))
+        rounded = (damped(p) * scale[pl.ds(p, 1), 0:1]).astype(bf16)
+        send_buf[p] = rounded
+        if k == side_reps:
+            start_of(j)[own_rows, :] = rounded
+
+    def send_all(j, ks):
+        for k in ks:
+            each(pieces(k, rep, 1 - side), functools.partial(send_in, j, k))
+
+    for k in far_ks:
+        round_rows(0, k)
+        send_all(0, [k])
+    send_all(0, near_ks)
+    for j in range(1, slots):
         for k in far_ks:
-            p = factor_of(j, target(k))
-            rounded = (damped(p) * scale[pl.ds(p, 1), 0:1]).astype(bf16)
-            send_buf[p] = rounded
-            if k == side_reps:
-                start_of(j)[own_rows, :] = rounded
-            each(pieces(k, rep, 1 - side), functools.partial(send_in, j, k))
-        for k in near_ks:
-            each(pieces(k, rep, 1 - side), functools.partial(send_in, j, k))
+            round_rows(j, k)
 
     def forward_copy(j, k, i, c):
         at = block_rows(blk, source(k))
@@ -239,6 +247,10 @@
         for k in range(reps):
             each(pieces(k, source(k), side), functools.partial(wait_forward, j, k))
         y0 = start_of(j)
+
+        @pl.when(j + 1 < slots)
+        def _():
+            send_all(j + 1, far_ks + near_ks)
 
         @pl.when(side == 0)
         def _():
@@ -305,6 +317,16 @@
                 eye = jnp.where(eye_rows == eye_cols + n * CHUNK, 3.0, 0.0)
                 step[:, cols(n)] = ((eye - moment) * 0.5).astype(bf16)
 
+        def make_step_rows(y, z, first, count):
+            first = pl.multiple_of(first, 16)
+            top = pl.multiple_of(blk * half + first, 16)
+            ids = top + lax.broadcasted_iota(jnp.int32, (count, CHUNK), 0)
+            for n in range(chunks):
+                moment = product(y[pl.ds(top, count), :], z, n)
+                at = n * CHUNK + lax.broadcasted_iota(jnp.int32, (count, CHUNK), 1)
+                eye = jnp.where(ids == at, 3.0, 0.0)
+                step[pl.ds(first, count), cols(n)] = ((eye - moment) * 0.5).astype(bf16)
+
         y, z, z_in = held[0].at[j], z1, []
         y_in = advance(z1.at[mine], y0, [], y, 0)
         ex = 1
@@ -315,8 +337,8 @@
             y_in = advance(step, y, y_in, y_next, ex + 1)
             y, z, z_in = y_next, z_next, z_in_next
             ex = ex + 2
-        make_step(y, z, z_in)
-
+        settle(z_in)
+        make_step_rows(y, z, side * far, far)
         for n in range(chunks):
             last_inv[j, :, cols(n)] = product(step[near_rows, :], z, n).astype(bf16)
         for k in near_ks:
@@ -326,6 +348,7 @@
         def _():
             forward_all(j + 1)
 
+        make_step_rows(y, z, (1 - side) * far, far)
         settle(y_in)
         for h in range(2):
             at = pl.ds(pl.multiple_of(h * half + side * narrow, LANES), wide)

time: 119 us -> 110 us (0.924)
  Pallas kernels: 112 us -> 103 us
    pallas_call x1, Pallas kernels: 112 us -> 103 us  [fused(): pl.pallas_call(functools.partial(kernel, reps), out_shape=(jax.ShapeDtype...]
where the time goes in v3:
time: 110 us
  Pallas kernels  103 us (94%)
  other arithmetic  5.48 us (5%)
    pallas_call x1, Pallas kernels, fused(): pl.pallas_call(functools.partial(kernel, reps), out_shape=(jax.ShapeDtype...  103 us
    div x1, other arithmetic, fused(): inv.astype(jnp.float32) / root_scale  5.48 us

profile of v3, /device:TPU:0, one launch (start us, length us, event | category | flops | bytes accessed | tf_op | source)
XLA Modules:
  0.0 110.1 jit_solution(14013773104875600852)
XLA Ops:
  0.6 103.2 %shard_map.41 = (bf16[8,80,1280]{2,1,0:T(8,128)(2,1)}, bf16[8,80,1280]{2,1,0:T(8,128)(2,1)}, f32[8,128]{1,0:T(8,128)}) custom-call(f32[8,80,1280]{2,1,0:T(8,128)} %fac_hbm.1, f32[8]{0:T(128)} %damp_ref.1), custom_call_target="tpu_custom_call" | custom-call | tf_op jit(solution)/shard_map/pallas_call | solution.py:393
  103.8 0.8 sqrt_reduce_fusion
  104.6 5.5 %convert_divide_fusion = (f32[8,80,1280]{2,1,0:T(8,128)}, f32[8,80,1280]{2,1,0:T(8,128)}) fusion(bf16[8,80,1280]{2,1,0:T(8,128)(2,1)} %get-tuple-element.7, f32[8]{0:T(128)S(1)} %sqrt_reduce_fusion, bf16[8,80,1280]{2,1,0:T(8,128)(2,1)} %get-tuple-element.5), kind=kLoop, calls=%fused_computation | loop fusion | flops 3276800 | bytes 9830432 | tf_op jit(solution)/shard_map/div | solution.py:430

commit v4 on v3

--- a/solution.py
+++ b/solution.py
@@ -15,10 +15,10 @@
 
 def kernel(
     reps, fac_hbm, damp_ref,
-    root_ref, inv_ref, norm_ref,
-    fac, part, scale, send_buf, start, held, z1, step, near_y, last_root, last_inv,
+    root_hbm, inv_hbm, norm_ref,
+    root_ref, inv_ref, fac, part, scale, send_buf, start, held, z1, step, near_y, last_root, last_inv,
     load_sem, sum_send, sum_recv, in_send, in_recv, fwd_send, fwd_recv,
-    ex_send, ex_recv, root_send, root_recv, inv_send, inv_recv,
+    ex_send, ex_recv, root_send, root_recv, inv_send, inv_recv, store_sem,
 ):
     grp = lax.axis_index("grp")
     rep = lax.axis_index("rep")
@@ -216,7 +216,8 @@
     eye_rows = blk * half + lax.broadcasted_iota(jnp.int32, (half, CHUNK), 0)
     eye_cols = lax.broadcasted_iota(jnp.int32, (half, CHUNK), 1)
 
-    parts = [(0, (chunks + 1) // 2), ((chunks + 1) // 2, chunks)]
+    whole = [(0, chunks)]
+    halves = [(0, (chunks + 1) // 2), ((chunks + 1) // 2, chunks)]
 
     def cols(n):
         return slice(n * CHUNK, (n + 1) * CHUNK)
@@ -284,8 +285,7 @@
 
         pending = []
 
-        def share(dst, ex, part):
-            first, last = parts[part]
+        def share(dst, ex, part, first, last):
             view = dst.at[mine, pl.ds(first * CHUNK, (last - first) * CHUNK)]
             copy = remote(
                 view, view, ex_send.at[j, ex, part], ex_recv.at[j, ex, part], rep, 1 - blk
@@ -301,13 +301,13 @@
         def product(lhs, rhs, n):
             return jnp.dot(lhs, rhs[:, cols(n)], preferred_element_type=f32)
 
-        def advance(lhs, rhs, arrivals, dst, ex):
+        def advance(lhs, rhs, arrivals, dst, ex, parts):
             settle(arrivals)
             shared = []
             for part, (first, last) in enumerate(parts):
                 for n in range(first, last):
                     dst[mine, cols(n)] = product(lhs[...], rhs, n).astype(bf16)
-                shared.append(share(dst, ex, part))
+                shared.append(share(dst, ex, part, first, last))
             return shared
 
         def make_step(y, z, arrivals):
@@ -328,13 +328,13 @@
                 step[pl.ds(first, count), cols(n)] = ((eye - moment) * 0.5).astype(bf16)
 
         y, z, z_in = held[0].at[j], z1, []
-        y_in = advance(z1.at[mine], y0, [], y, 0)
+        y_in = advance(z1.at[mine], y0, [], y, 0, whole)
         ex = 1
         for _ in range(ITERS - 2):
             make_step(y, z, z_in)
             z_next, y_next = held[ex].at[j], held[ex + 1].at[j]
-            z_in_next = advance(step, z, [], z_next, ex)
-            y_in = advance(step, y, y_in, y_next, ex + 1)
+            z_in_next = advance(step, z, [], z_next, ex, halves)
+            y_in = advance(step, y, y_in, y_next, ex + 1, whole)
             y, z, z_in = y_next, z_next, z_in_next
             ex = ex + 2
         settle(z_in)
@@ -372,11 +372,47 @@
     for j in range(slots):
         for k in range(1, reps):
             each(pieces(k, rep, 1 - side), functools.partial(wait_in, j, k))
+
+    stores = []
+
+    def keep(ref, hbm, f, which):
+        store = pltpu.make_async_copy(ref.at[f], hbm.at[f], store_sem.at[which, len(stores)])
+        store.start()
+        stores.append(store)
+
     for j in range(slots):
+        keep(inv_ref, inv_hbm, factor_of(j, rep), 0)
         for k in near_ks:
             inv_copy(j, k).wait()
-        for k, flip in root_ks:
-            root_copy(j, k, flip).wait()
+            keep(inv_ref, inv_hbm, factor_of(j, source(k)), 0)
+        for k in [0] + near_ks:
+            for flip in range(2):
+                if (k, flip) in root_ks:
+                    root_copy(j, k, flip).wait()
+            keep(root_ref, root_hbm, factor_of(j, source(k)), 1)
+    for store in stores:
+        store.wait()
+
+
+def finish(root_hbm, inv_hbm, norm_ref, root_out, inv_out, held, wide, load_sem, store_sem):
+    facs = root_hbm.shape[0]
+    jobs = []
+    for f in range(facs):
+        for which, (src, dst) in enumerate(((inv_hbm, inv_out), (root_hbm, root_out))):
+            load = pltpu.make_async_copy(src.at[f], held.at[which, f], load_sem.at[which, f])
+            load.start()
+            jobs.append((which, f, load, dst))
+    stores = []
+    for which, f, load, dst in jobs:
+        load.wait()
+        scale = jnp.sqrt(norm_ref[f : f + 1, 0:1])
+        x = held[which, f].astype(jnp.float32)
+        wide[which, f] = x * scale if which else x / scale
+        store = pltpu.make_async_copy(wide.at[which, f], dst.at[f], store_sem.at[which, f])
+        store.start()
+        stores.append(store)
+    for store in stores:
+        store.wait()
 
 
 def fused(mesh, factors, damping):
@@ -388,6 +424,7 @@
     wide = -(-(half // 2) // LANES) * LANES
     dma = pltpu.SemaphoreType.DMA
     vmem = pl.BlockSpec(memory_space=pltpu.VMEM)
+    hbm = pl.BlockSpec(memory_space=pl.ANY)
     exchanges = 2 * ITERS - 3
     bf16 = jnp.bfloat16
     root, inv, norm = pl.pallas_call(
@@ -401,8 +438,10 @@
             pl.BlockSpec(memory_space=pl.ANY),
             pl.BlockSpec(memory_space=pltpu.SMEM),
         ],
-        out_specs=(vmem, vmem, vmem),
+        out_specs=(hbm, hbm, vmem),
         scratch_shapes=[
+            pltpu.VMEM(factors.shape, bf16),
+            pltpu.VMEM(factors.shape, bf16),
             pltpu.VMEM(factors.shape, jnp.float32),
             pltpu.VMEM((members, facs, LANES), jnp.float32),
             pltpu.VMEM((facs, LANES), jnp.float32),
@@ -421,13 +460,24 @@
             dma((slots, exchanges, 2)), dma((slots, exchanges, 2)),
             dma((slots, reps, 2)), dma((slots, reps, 2)),
             dma((slots, reps)), dma((slots, reps)),
+            dma((2, 2 * facs)),
         ],
         compiler_params=pltpu.CompilerParams(
             collective_id=0, has_side_effects=True, vmem_limit_bytes=63 * 2**20
         ),
     )(factors, damping)
-    root_scale = jnp.sqrt(norm[:, :1])[:, :, None]
-    return root.astype(jnp.float32) * root_scale, inv.astype(jnp.float32) / root_scale
+    whole = jax.ShapeDtypeStruct(factors.shape, jnp.float32)
+    return pl.pallas_call(
+        finish,
+        out_shape=(whole, whole),
+        in_specs=[hbm, hbm, vmem],
+        out_specs=(hbm, hbm),
+        scratch_shapes=[
+            pltpu.VMEM((2,) + factors.shape, bf16),
+            pltpu.VMEM((2,) + factors.shape, jnp.float32),
+            dma((2, facs)), dma((2, facs)),
+        ],
+    )(root, inv, norm)
 
 
 def plain(factors, damping):

time: 110 us -> 108 us (0.982)
  other arithmetic: 5.48 us -> 0 us
  Pallas kernels: 103 us -> 107 us
    div x1 -> x0, other arithmetic: 5.48 us -> none  [fused(): inv.astype(jnp.float32) / root_scale]
    pallas_call x0 -> x1, Pallas kernels: none -> 4.68 us  [fused(): pl.pallas_call(finish, out_shape=(whole, whole), in_specs=[hbm, hbm, vmem...]
where the time goes in v4:
time: 108 us
  Pallas kernels  107 us (99%)
    pallas_call x1, Pallas kernels, fused(): pl.pallas_call(functools.partial(kernel, reps), out_shape=(jax.ShapeDtype...  102 us
    pallas_call x1, Pallas kernels, fused(): pl.pallas_call(finish, out_shape=(whole, whole), in_specs=[hbm, hbm, vmem...  4.68 us

profile of v4, /device:TPU:0, one launch (start us, length us, event | category | flops | bytes accessed | tf_op | source)
XLA Modules:
  0.0 107.8 jit_solution(16556334496621526345)
XLA Ops:
  0.6 102.3 %shard_map.41 = (bf16[8,80,1280]{2,1,0:T(8,128)(2,1)}, bf16[8,80,1280]{2,1,0:T(8,128)(2,1)}, f32[8,128]{1,0:T(8,128)}) custom-call(f32[8,80,1280]{2,1,0:T(8,128)} %fac_hbm.1, f32[8]{0:T(128)} %damp_ref.1), custom_call_target="tpu_custom_call" | custom-call | tf_op jit(solution)/shard_map/pallas_call | solution.py:430
  103.0 4.7 %shard_map.42 = (f32[8,80,1280]{2,1,0:T(8,128)}, f32[8,80,1280]{2,1,0:T(8,128)}) custom-call(bf16[8,80,1280]{2,1,0:T(8,128)(2,1)} %get-tuple-element.5.root_hbm, bf16[8,80,1280]{2,1,0:T(8,128)(2,1)} %get-tuple-element.6.inv_hbm, f32[8,128]{1,0:T(8,128)} %get-tuple-element.7.norm_ref), custom_call_target="tpu_custom_call" | custom-call | tf_op jit(solution)/shard_map/pallas_call | solution.py:470

commit v5 on v4

--- a/solution.py
+++ b/solution.py
@@ -16,7 +16,7 @@
 def kernel(
     reps, fac_hbm, damp_ref,
     root_hbm, inv_hbm, norm_ref,
-    root_ref, inv_ref, fac, part, scale, send_buf, start, held, z1, step, near_y, last_root, last_inv,
+    root_ref, inv_ref, fac, part, scale, send_buf, start, held, z1, step, last_root, last_inv,
     load_sem, sum_send, sum_recv, in_send, in_recv, fwd_send, fwd_recv,
     ex_send, ex_recv, root_send, root_recv, inv_send, inv_recv, store_sem,
 ):
@@ -71,7 +71,11 @@
         acc = col[:, :LANES]
         for c in range(1, order // LANES):
             acc = acc + col[:, c * LANES : (c + 1) * LANES]
-        part[pl.ds(rank, 1), f : f + 1, :] = acc[None]
+        norm_ref[f : f + 1, :] = acc
+    at_lane = lax.broadcasted_iota(jnp.int32, (facs, LANES), 1)
+    here = lax.broadcasted_iota(jnp.int32, (facs, LANES), 0) == at_lane
+    own_sums = jnp.sum(norm_ref[...], axis=1, keepdims=True)
+    part[rank] = jnp.sum(jnp.where(here, own_sums, 0.0), axis=0, keepdims=True)
     pl.semaphore_wait(barrier, members - 1)
 
     sums = []
@@ -85,7 +89,7 @@
     total = part[0]
     for q in range(1, members):
         total = total + part[q]
-    norm = jnp.sqrt(jnp.sum(total, axis=1, keepdims=True))
+    norm = jnp.sqrt(jnp.sum(jnp.where(here, total, 0.0), axis=1, keepdims=True))
     norm_ref[...] = jnp.broadcast_to(norm, norm_ref.shape)
     scale[...] = jnp.broadcast_to(1.0 / norm, scale.shape)
 
@@ -277,12 +281,9 @@
                     t = t.astype(f32).T[:far, :]
                     y0[at] = fill(t, y0[at], 0, half - miss, True)
 
-        for q in range(members):
-            at = slice(q * rows, (q + 1) * rows)
-            ids = q * rows + lax.broadcasted_iota(jnp.int32, (rows, order), 0)
-            eye = ids == lax.broadcasted_iota(jnp.int32, (rows, order), 1)
-            z1[at, :] = ((jnp.where(eye, 3.0, 0.0) - y0[at, :].astype(f32)) * 0.5).astype(bf16)
-
+        for n in range(chunks):
+            eye = jnp.where(eye_rows == eye_cols + n * CHUNK, 3.0, 0.0)
+            step[:, cols(n)] = ((eye - y0[mine, cols(n)].astype(f32)) * 0.5).astype(bf16)
         pending = []
 
         def share(dst, ex, part, first, last):
@@ -328,7 +329,13 @@
                 step[pl.ds(first, count), cols(n)] = ((eye - moment) * 0.5).astype(bf16)
 
         y, z, z_in = held[0].at[j], z1, []
-        y_in = advance(z1.at[mine], y0, [], y, 0, whole)
+        y_in = advance(step, y0, [], y, 0, whole)
+        for q in range(members):
+            at = slice(q * rows, (q + 1) * rows)
+            ids = q * rows + lax.broadcasted_iota(jnp.int32, (rows, order), 0)
+            eye = ids == lax.broadcasted_iota(jnp.int32, (rows, order), 1)
+            z1[at, :] = ((jnp.where(eye, 3.0, 0.0) - y0[at, :].astype(f32)) * 0.5).astype(bf16)
+
         ex = 1
         for _ in range(ITERS - 2):
             make_step(y, z, z_in)
@@ -352,9 +359,9 @@
         settle(y_in)
         for h in range(2):
             at = pl.ds(pl.multiple_of(h * half + side * narrow, LANES), wide)
-            near_y[:, h * wide : (h + 1) * wide] = y[:, at]
+            z1[:, h * wide : (h + 1) * wide] = y[:, at]
         for n in range(2 * wide // CHUNK):
-            out = product(step[...], near_y, n)
+            out = product(step[...], z1, n)
             last_root[j, cols(n), :] = out.T.astype(bf16)
         for k, flip in root_ks:
             root_copy(j, k, flip).start()
@@ -443,14 +450,13 @@
             pltpu.VMEM(factors.shape, bf16),
             pltpu.VMEM(factors.shape, bf16),
             pltpu.VMEM(factors.shape, jnp.float32),
-            pltpu.VMEM((members, facs, LANES), jnp.float32),
+            pltpu.VMEM((members, 1, LANES), jnp.float32),
             pltpu.VMEM((facs, LANES), jnp.float32),
             pltpu.VMEM(factors.shape, bf16),
             pltpu.VMEM((slots, order, order), bf16),
             [pltpu.VMEM((slots, order, order), bf16) for _ in range(exchanges)],
             pltpu.VMEM((order, order), bf16),
             pltpu.VMEM((half, order), bf16),
-            pltpu.VMEM((order, 2 * wide), bf16),
             pltpu.VMEM((slots, 2 * wide, half), bf16),
             pltpu.VMEM((slots, half // 2, order), bf16),
             dma((facs,)),

time: 108 us -> 107 us (level)
    pallas_call x1, Pallas kernels: 102 us -> 101 us  [fused(): pl.pallas_call(functools.partial(kernel, reps), out_shape=(jax.ShapeDtype...]
where the time goes in v5:
time: 107 us; the launch traced here: 106 us
  Pallas kernels  106 us (99%)
    pallas_call x1, Pallas kernels, fused(): pl.pallas_call(functools.partial(kernel, reps), out_shape=(jax.ShapeDtype...  101 us
    pallas_call x1, Pallas kernels, fused(): pl.pallas_call(finish, out_shape=(whole, whole), in_specs=[hbm, hbm, vmem...  4.68 us

profile of v5, /device:TPU:0, one launch (start us, length us, event | category | flops | bytes accessed | tf_op | source)
XLA Modules:
  0.0 106.3 jit_solution(8921039384119417706)
XLA Ops:
  0.6 100.9 %shard_map.41 = (bf16[8,80,1280]{2,1,0:T(8,128)(2,1)}, bf16[8,80,1280]{2,1,0:T(8,128)(2,1)}, f32[8,128]{1,0:T(8,128)}) custom-call(f32[8,80,1280]{2,1,0:T(8,128)} %fac_hbm.1, f32[8]{0:T(128)} %damp_ref.1), custom_call_target="tpu_custom_call" | custom-call | tf_op jit(solution)/shard_map/pallas_call | solution.py:437
  101.5 4.7 %shard_map.42 = (f32[8,80,1280]{2,1,0:T(8,128)}, f32[8,80,1280]{2,1,0:T(8,128)}) custom-call(bf16[8,80,1280]{2,1,0:T(8,128)(2,1)} %get-tuple-element.5.root_hbm, bf16[8,80,1280]{2,1,0:T(8,128)(2,1)} %get-tuple-element.6.inv_hbm, f32[8,128]{1,0:T(8,128)} %get-tuple-element.7.norm_ref), custom_call_target="tpu_custom_call" | custom-call | tf_op jit(solution)/shard_map/pallas_call | solution.py:476
